TPU v7x, 256 devices: a 8x8x2 block of a 8x8x16 slice. The times are simulated.
256 devices in a mesh: groups: 2 (over z), adapter: 16 (over x, core), tensor: 8 (over y).
Axes of the slice: x: 8, y: 8, z: 2, core: 2. Of those that a mesh axis runs over, the one named last changes fastest.
The devices are a block of a 8x8x16 slice.
Arguments:
- tokens: bfloat16 [8192, 8192], P(('groups', 'adapter'), 'tensor'), parts along dimension 0, may hold values from -6 to 6
- query_weight: bfloat16 [8192, 8192], P('tensor', 'adapter'), may hold values from -0.0625 to 0.0625
- adapter_down_weight: bfloat16 [512, 16, 8192], P('adapter', None, 'tensor'), may hold values from -0.0625 to 0.0625
- adapter_up_weight: bfloat16 [512, 16, 8192], P('adapter'), may hold values from -1.5 to 1.5
- block_adapter_ids: int32 [64], P('groups'), parts along dimension 0, may hold values from 0 to 511, as said below
- block_live_count: int32 [64], P('groups'), parts along dimension 0, may hold values from 1 to 128
- adapter_slot_index: int32 [1024], P('groups'), parts along dimension 0, may hold values from 0 to 511, as said below
Outputs:
- query: bfloat16 [8192, 8192], P(('groups', 'tensor'), 'adapter'), parts along dimension 0
There are 2 independent parts, one for each index of `groups`. A program takes and returns all parts, laid end to end along the dimension named above; an argument that names none is the same for every part. Nothing has to cross between parts.
Inputs may be any that keep to these rules, and one draw needn't show every extreme that they name: Counting blocks by the owner range adapter_slot_index[block_adapter_ids[k]] // 32, no owner has more than 4 blocks, and one owner has exactly 4 in every draw. `adapter_slot_index`: A permutation: each slot holds exactly one adapter.
All inputs are finite; a program needn't handle non-finite values.
Results may differ from a plain program's by a relative error of at most 0.014.
Values may be sent and summed in bfloat16 or wider, within the bound.
A program may use at most 128 MiB of HBM per device.

v0:
```python
import jax
import jax.numpy as jnp
from jax import lax
from jax.sharding import PartitionSpec as P

BLOCK = 128
adapter_scale = 2.0


def block_plan(block_adapter_ids, adapter_slot_index, owners, adapters_per_device, capacity):
    adapters = adapter_slot_index.shape[0]
    picked = block_adapter_ids[:, None] == jnp.arange(adapters, dtype=jnp.int32)[None, :]
    block_slot_index = jnp.sum(jnp.where(picked, adapter_slot_index[None, :], 0), axis=1)
    owner_of = block_slot_index // adapters_per_device
    local_slot = block_slot_index % adapters_per_device
    hit_table = (owner_of[:, None] == jnp.arange(owners, dtype=jnp.int32)[None, :]).astype(
        jnp.int32
    )
    before = jnp.cumsum(hit_table, axis=0) - hit_table
    order_in = jnp.sum(before * hit_table, axis=1)
    return (owner_of, local_slot, order_in, owner_of * capacity + order_in)


def on_device(
    tokens,
    query_weight,
    adapter_down_weight,
    adapter_up_weight,
    block_adapter_ids,
    block_live_count,
    adapter_slot_index,
):
    owners = lax.axis_size("adapter")
    my_index = lax.axis_index("adapter")
    tok_dev = tokens.shape[0]
    features = tokens.shape[1]
    adapters_per_device = adapter_down_weight.shape[0]
    rank_width = adapter_down_weight.shape[1]
    blocks = block_adapter_ids.shape[0]
    blk_dev = blocks // owners
    capacity = 2 * blk_dev
    token_row_count = tok_dev * owners
    output_columns = query_weight.shape[1]
    owner_of, local_slot, order_in, packed = block_plan(
        block_adapter_ids, adapter_slot_index, owners, adapters_per_device, capacity
    )
    seat_ids = jnp.arange(capacity, dtype=jnp.int32)
    matches = (owner_of[None, :] == my_index) & (order_in[None, :] == seat_ids[:, None])
    filled = jnp.any(matches, axis=1)
    match_int = matches.astype(jnp.int32)
    local_adapter_rows = jnp.sum(match_int * local_slot[None, :], axis=1)
    token_keep_mask = filled.astype(jnp.bfloat16)
    positions = jnp.arange(BLOCK, dtype=jnp.int32)
    up_weight_packed = (
        jnp.take(adapter_up_weight, local_adapter_rows, axis=0) * token_keep_mask[:, None, None]
    )
    up_recv = lax.all_to_all(up_weight_packed, "adapter", split_axis=2, concat_axis=0, tiled=True)
    down_weight_packed = (
        jnp.take(adapter_down_weight, local_adapter_rows, axis=0) * token_keep_mask[:, None, None]
    )
    down_all = lax.all_gather(down_weight_packed, "adapter", axis=0, tiled=True)
    own_packed = lax.dynamic_slice_in_dim(packed, my_index * blk_dev, blk_dev)
    own_live = lax.dynamic_slice_in_dim(block_live_count, my_index * blk_dev, blk_dev)
    down_own = jnp.take(down_all, own_packed, axis=0)
    live_own = (positions[None, :] < own_live[:, None]).astype(jnp.float32)
    shrunk_own = jnp.einsum(
        "ksd,krd->ksr",
        tokens.reshape(blk_dev, BLOCK, features),
        down_own,
        preferred_element_type=jnp.float32,
    )
    shrunk_own = (
        (shrunk_own * live_own[:, :, None]).astype(jnp.bfloat16).reshape(tok_dev, rank_width)
    )
    token_piece = lax.all_gather(tokens, "adapter", axis=0, tiled=True)
    shrunk_piece = lax.all_gather(shrunk_own, "adapter", axis=0, tiled=True)
    query_product = jnp.dot(token_piece, query_weight, preferred_element_type=jnp.float32)
    up_weight_blocks = jnp.take(up_recv, packed, axis=0)
    adapter_output = jnp.einsum(
        "ksr,krf->ksf",
        shrunk_piece.reshape(blocks, BLOCK, rank_width),
        up_weight_blocks,
        preferred_element_type=jnp.float32,
    )
    partial_output = query_product + adapter_scale * adapter_output.reshape(
        token_row_count, output_columns
    )
    summed = lax.psum_scatter(
        partial_output.astype(jnp.bfloat16), "tensor", scatter_dimension=0, tiled=True
    )
    return summed


def solution(mesh):
    placed = (
        P(("groups", "adapter"), "tensor"),
        P("tensor", "adapter"),
        P("adapter", None, "tensor"),
        P("adapter", None, None),
        P("groups"),
        P("groups"),
        P("groups"),
    )
    return jax.shard_map(
        on_device,
        mesh=mesh,
        in_specs=placed,
        out_specs=P(("groups", "tensor"), "adapter"),
        check_vma=False,
    )
```

profile of v0, /device:TPU:513, one launch (start us, length us, event | category | flops | bytes accessed | tf_op | source)
XLA Modules:
  0.0 212.7 jit_solution(3576047556961893171)
XLA Ops:
  6.5 0.0 copy-start
  6.6 0.0 all-gather.5.cloned.1.call-start
  6.6 1.0 select_reduce_fusion
  7.5 0.1 fusion.11
  7.6 0.1 reduce_window_sum.11
  7.7 0.2 select_reduce_fusion.1
  7.9 0.1 fusion.13
  8.0 0.1 select_reduce_fusion.2
  8.1 1.8 gather_fusion
  9.9 0.7 select_multiply_fusion.1
  10.7 0.1 all-gather.5.cloned.1.call-update
  10.7 0.1 all-gather.3.cloned.1.call-start
  10.8 0.7 all-gather.3.cloned.1.call-update
  11.6 4.0 %gather_fusion.2 = bf16[4,16,8192]{2,1,0:T(8,128)(2,1)S(1)} fusion(bf16[32,16,8192]{2,1,0:T(8,128)(2,1)} %param.10, s32[1024]{0:T(1024)S(1)} %pad_clamp_fusion.2), kind=kCustom, calls=%fused_computation.2 | custom fusion | bytes 2097168 | tf_op jit(solution)/shard_map/jit(_take)/gather | solution.py:55
  15.6 0.2 select_multiply_fusion
  15.7 0.0 copy-start.2
  15.7 8.3 %copy.23 = bf16[4,16,8192]{1,0,2:T(4,128)(2,1)} copy(bf16[4,16,8192]{2,1,0:T(8,128)(2,1)S(1)} %select_multiply_fusion) | data formatting | bytes 2097152 | tf_op jit(solution)/shard_map/mul | solution.py:55
  24.0 11.2 %reshape.207 = bf16[16,2,16384]{2,1,0:T(2,128)(2,1)} reshape(bf16[8192,4,16]{2,1,0:T(4,128)(2,1)} %bitcast.48) | data formatting | bytes 2097152
  35.3 23.9 %all-to-all-start = ((bf16[16,2,16384]{2,1,0:T(2,128)(2,1)}), bf16[16,2,16384]{2,1,0:T(2,128)(2,1)S(1)}, u32[]{:S(2)}, u32[]{:S(2)}) async-start(bf16[16,2,16384]{2,1,0:T(2,128)(2,1)} %reshape.207), calls=%async_computation | async-start | bytes 2097152 | tf_op jit(solution)/shard_map/all_to_all | solution.py:57
  59.2 0.1 reduce-scatter.2.cloned.1.call-start
  59.2 0.0 copy-done.2
  59.2 0.1 dynamic_slice.7
  59.3 0.1 compare_and_fusion.2
  59.4 0.1 compare_convert_fusion
  59.5 0.0 copy-start.1
  59.5 27.7 %all-to-all-done = bf16[16,2,16384]{2,1,0:T(2,128)(2,1)S(1)} async-done(((bf16[16,2,16384]{2,1,0:T(2,128)(2,1)}), bf16[16,2,16384]{2,1,0:T(2,128)(2,1)S(1)}, u32[]{:S(2)}, u32[]{:S(2)}) %all-to-all-start) | async-done | bytes 1048608 | tf_op jit(solution)/shard_map/all_to_all | solution.py:57
  87.2 7.6 %reshape.208 = bf16[8192,4,16]{2,1,0:T(4,128)(2,1)} reshape(bf16[16,2,16384]{2,1,0:T(2,128)(2,1)S(1)} %all-to-all-done) | data formatting | bytes 2097152
  94.8 10.8 %copy.28 = bf16[4,16,16,512]{3,1,0,2:T(8,128)(2,1)S(1)} copy(bf16[4,16,16,512]{1,0,3,2:T(4,128)(2,1)} %bitcast.49) | data formatting | bytes 2097152 | tf_op jit(solution)/shard_map/all_to_all | solution.py:57
  105.6 0.6 gather_fusion.3
  106.2 0.0 all-gather.5.cloned.1.call-done
  106.2 2.2 %gather_fusion.1 = bf16[2,16,1024]{2,1,0:T(8,128)(2,1)S(1)} fusion(bf16[64,16,1024]{2,1,0:T(8,128)(2,1)} %all-gather.5.cloned.1.call-done, s32[1024]{0:T(1024)S(1)} %pad_clamp_fusion.1), kind=kCustom, calls=%fused_computation.1 | custom fusion | bytes 131080 | tf_op jit(solution)/shard_map/jit(_take)/gather | solution.py:64
  108.4 0.0 copy-done.1
  108.4 0.3 fusion.2
  108.7 17.2 %all_gather.11 = bf16[4096,16]{0,1:T(8,128)(2,1)S(1)} all-gather(bf16[256,16]{0,1:T(8,128)(2,1)S(1)} %bitcast.52), channel_id=1, replica_groups=mesh['groups'=2,'adapter'=16,'tensor'=8] {'adapter'}, dimensions={0}, use_global_device_ids=true | all-gather | bytes 139264 | tf_op jit(solution)/shard_map/all_gather | solution.py:76
  125.9 4.5 %broadcast_multiply_fusion = f32[32,128,512]{2,1,0:T(8,128)} fusion(bf16[32,16,512]{2,1,0:T(8,128)(2,1)S(1)} %gather_fusion.3, pred[32]{0:T(512)(128)(4,1)S(1)} %get-tuple-element.7, bf16[4096,16]{0,1:T(8,128)(2,1)S(1)} %all_gather.11), kind=kOutput, calls=%fused_computation.6 | convolution fusion | flops 69468160 | bytes 9044000 | tf_op jit(solution)/shard_map/ksr,krf->ksf/dot_general | solution.py:79
  130.4 9.4 %all-gather.3.cloned.1.call-done = bf16[4096,1024]{1,0:T(8,128)(2,1)} async-done(((bf16[256,1024]{1,0:T(8,128)(2,1)}), bf16[4096,1024]{1,0:T(8,128)(2,1)}) %all-gather.3.cloned.1.call-update) | async-done | bytes 8388624 | tf_op jit(solution)/shard_map/all_gather | solution.py:75
  139.8 0.0 copy-done
  139.8 10.7 %fusion = bf16[4096,512]{1,0:T(8,128)(2,1)} fusion(f32[32,128,512]{2,1,0:T(8,128)} %broadcast_multiply_fusion, bf16[4096,1024]{1,0:T(8,128)(2,1)} %all-gather.3.cloned.1.call-done, bf16[1024,512]{1,0:T(8,128)(2,1)S(1)} %copy-done), kind=kOutput, calls=%fused_computation.5 | convolution fusion | flops 4299161600 | bytes 22020096 | tf_op jit(solution)/shard_map/dot_general | solution.py:77
  150.5 0.1 reduce-scatter.2.cloned.1.call-update
  150.6 55.6 %reduce-scatter.2.cloned.1.call-done = bf16[512,512]{1,0:T(8,128)(2,1)} async-done(((bf16[4096,512]{1,0:T(8,128)(2,1)}), bf16[512,512]{1,0:T(8,128)(2,1)}) %reduce-scatter.2.cloned.1.call-update) | async-done | bytes 524304 | tf_op jit(solution)/shard_map/reduce_scatter | solution.py:88
  (11 shorter events, 0.1 us)
Async XLA Ops:
  6.5 133.2 %copy-start = (bf16[1024,512]{1,0:T(8,128)(2,1)S(1)}, bf16[1024,512]{1,0:T(8,128)(2,1)}, u32[]{:S(2)}) copy-start(bf16[1024,512]{1,0:T(8,128)(2,1)} %param.8) | copy-start | bytes 3145732
  6.6 99.6 %all-gather.5.cloned.1.call-start = ((), (), s32[]{:S(2)}) async-start(), calls=%async_computation.3 | async-start | bytes 2228224 | tf_op jit(solution)/shard_map/all_gather | solution.py:61
  10.7 129.0 %all-gather.3.cloned.1.call-start = ((), (), s32[]{:S(2)}) async-start(), calls=%async_computation.2 | async-start | bytes 8912896 | tf_op jit(solution)/shard_map/all_gather | solution.py:75
  15.7 43.5 %copy-start.2 = (s32[32]{0:T(128)S(1)}, s32[32]{0:T(128)}, u32[]{:S(2)}) copy-start(s32[32]{0:T(128)} %param.12) | copy-start | bytes 388
  35.3 51.9 %all-to-all-start = ((bf16[16,2,16384]{2,1,0:T(2,128)(2,1)}), bf16[16,2,16384]{2,1,0:T(2,128)(2,1)S(1)}, u32[]{:S(2)}, u32[]{:S(2)}) async-start(bf16[16,2,16384]{2,1,0:T(2,128)(2,1)} %reshape.207), calls=%async_computation | async-start | bytes 2097152 | tf_op jit(solution)/shard_map/all_to_all | solution.py:57
  59.2 147.0 %reduce-scatter.2.cloned.1.call-start = ((), (), s32[]{:S(2)}) async-start(), calls=%async_computation.4 | async-start | bytes 4718592 | tf_op jit(solution)/shard_map/reduce_scatter | solution.py:88
  59.5 48.9 %copy-start.1 = (bf16[256,1024]{1,0:T(8,128)(2,1)S(1)}, bf16[256,1024]{1,0:T(8,128)(2,1)}, u32[]{:S(2)}) copy-start(bf16[256,1024]{1,0:T(8,128)(2,1)} %param.7) | copy-start | bytes 1572868
Sparse Core Ops, SparseCore 0:
  10.9 65.9 all-gather.4
  78.7 61.0 all-gather.2
  150.7 55.4 reduce-scatter.1
where the time goes:
time: 213 us
  waiting for transfers between devices  93.5 us (44%)
  local copies, waits for them, and re-layouts  46.6 us (22%)
  starting transfers between devices  24 us (11%)
  blocking collectives  17.2 us (8%)
  matrix products  15.5 us (7%)
  between operations  13.3 us (6%)
  other arithmetic  2.65 us (1%)
    reduce_scatter x1, waiting for transfers between devices, on_device(): lax.psum_scatter(partial_output.astype(jnp.bfloat16), 'tensor', scatter_d...  55.6 us
    all_to_all x1, waiting for transfers between devices, on_device(): lax.all_to_all(up_weight_packed, 'adapter', split_axis=2, concat_axis=0,...  27.7 us
    all_to_all x1, starting transfers between devices, on_device(): lax.all_to_all(up_weight_packed, 'adapter', split_axis=2, concat_axis=0,...  23.9 us
    unnamed x8, local copies, waits for them, and re-layouts  18.9 us
    all_gather x1, blocking collectives, on_device(): shrunk_piece = lax.all_gather(shrunk_own, 'adapter', axis=0, tiled=True)  17.2 us
    all_to_all x1, local copies, waits for them, and re-layouts, on_device(): lax.all_to_all(up_weight_packed, 'adapter', split_axis=2, concat_axis=0,...  10.8 us
    dot_general x1, matrix products, on_device(): jnp.dot(token_piece, query_weight, preferred_element_type=jnp.float32)  10.7 us
    all_gather x1, waiting for transfers between devices, on_device(): token_piece = lax.all_gather(tokens, 'adapter', axis=0, tiled=True)  9.36 us
  transfers between devices with their start and end apart: 4, of which 3 were waited for; matrix products, arithmetic and copies ran while one was open for 23% of the time, Pallas kernels for 0%

commit v1 on v0

--- a/solution.py
+++ b/solution.py
@@ -54,7 +54,13 @@
     up_weight_packed = (
         jnp.take(adapter_up_weight, local_adapter_rows, axis=0) * token_keep_mask[:, None, None]
     )
-    up_recv = lax.all_to_all(up_weight_packed, "adapter", split_axis=2, concat_axis=0, tiled=True)
+    push_series_all_for = lambda row_axis, original: jnp.concatenate(
+        lax.all_to_all(
+            jnp.stack(jnp.split(original, lax.axis_size(row_axis), 2), 0), row_axis, 0, 0
+        ),
+        0,
+    )
+    up_recv = push_series_all_for("adapter", up_weight_packed)
     down_weight_packed = (
         jnp.take(adapter_down_weight, local_adapter_rows, axis=0) * token_keep_mask[:, None, None]
     )

time: 213 us -> 215 us (level)
  waiting for transfers between devices: 93.5 us -> 125 us
  local copies, waits for them, and re-layouts: 46.6 us -> 18.5 us
    all_gather x1, waiting for transfers between devices: 9.36 us -> 35.5 us  [on_device(): token_piece = lax.all_gather(tokens, 'adapter', axis=0, tiled=True)]
    all_to_all x1 -> x0, local copies, waits for them, and re-layouts: 10.8 us -> none  [on_device(): lax.all_to_all(up_weight_packed, 'adapter', split_axis=2, concat_axis=0,...]
    unnamed x8 -> x21, local copies, waits for them, and re-layouts: 18.9 us -> 9.34 us
    mul x1 -> x0, local copies, waits for them, and re-layouts: 8.29 us -> none  [on_device(): jnp.take(adapter_up_weight, local_adapter_rows, axis=0)]
    all_to_all x1, waiting for transfers between devices: 27.7 us -> 32.7 us  [on_device(): lax.all_to_all(jnp.stack(jnp.split(original, lax.axis_size(row_axis), 2),...]
  transfers between devices with their start and end apart: 4 -> 4, of which waited for: 3 -> 3; matrix products, arithmetic and copies ran while one was open for 23% -> 10% of each run, Pallas kernels for 0% -> 0%
where the time goes in v1:
time: 215 us; the launch traced here: 214 us
  waiting for transfers between devices  125 us (58%)
  starting transfers between devices  24 us (11%)
  local copies, waits for them, and re-layouts  18.5 us (9%)
  matrix products  15.6 us (7%)
  blocking collectives  15.4 us (7%)
  between operations  13.3 us (6%)
  other arithmetic  2.68 us (1%)
    reduce_scatter x1, waiting for transfers between devices, on_device(): lax.psum_scatter(partial_output.astype(jnp.bfloat16), 'tensor', scatter_d...  55.6 us
    all_gather x1, waiting for transfers between devices, on_device(): token_piece = lax.all_gather(tokens, 'adapter', axis=0, tiled=True)  35.5 us
    all_to_all x1, waiting for transfers between devices, on_device(): lax.all_to_all(jnp.stack(jnp.split(original, lax.axis_size(row_axis), 2),...  32.7 us
    all_to_all x1, starting transfers between devices, on_device(): lax.all_to_all(jnp.stack(jnp.split(original, lax.axis_size(row_axis), 2),...  23.9 us
    all_gather x1, blocking collectives, on_device(): shrunk_piece = lax.all_gather(shrunk_own, 'adapter', axis=0, tiled=True)  15.4 us
    dot_general x1, matrix products, on_device(): jnp.dot(token_piece, query_weight, preferred_element_type=jnp.float32)  10.8 us
    unnamed x21, local copies, waits for them, and re-layouts  9.34 us
    dot_general x1, matrix products, on_device(): jnp.einsum('ksr,krf->ksf', shrunk_piece.reshape(blocks, BLOCK, rank_width...  4.51 us
  transfers between devices with their start and end apart: 4, of which 3 were waited for; matrix products, arithmetic and copies ran while one was open for 10% of the time, Pallas kernels for 0%

profile of v1, /device:TPU:513, one launch (start us, length us, event | category | flops | bytes accessed | tf_op | source)
XLA Modules:
  0.0 214.2 jit_solution(5774402844650574217)
XLA Ops:
  6.5 0.0 copy-start
  6.6 0.0 all-gather.5.cloned.1.call-start
  6.6 1.0 select_reduce_fusion
  7.6 0.1 fusion.27
  7.7 0.1 reduce_window_sum.11
  7.7 0.2 select_reduce_fusion.1
  7.9 0.1 fusion.29
  8.0 0.1 select_reduce_fusion.2
  8.2 1.8 gather_fusion
  10.0 0.7 select_multiply_fusion.1
  10.7 0.1 all-gather.5.cloned.1.call-update
  10.8 0.1 all-gather.3.cloned.1.call-start
  10.9 0.7 all-gather.3.cloned.1.call-update
  11.6 4.0 %gather_fusion.2 = bf16[4,16,8192]{2,1,0:T(8,128)(2,1)S(1)} fusion(bf16[32,16,8192]{2,1,0:T(8,128)(2,1)} %param.10, s32[1024]{0:T(1024)S(1)} %pad_clamp_fusion.2), kind=kCustom, calls=%fused_computation.2 | custom fusion | bytes 2097168 | tf_op jit(solution)/shard_map/jit(_take)/gather | solution.py:55
  15.6 0.2 select_multiply_fusion
  15.8 0.6 fusion.23
  16.4 0.6 fusion.22
  17.0 0.6 fusion.21
  17.6 0.6 fusion.20
  18.3 0.6 fusion.19
  18.9 0.6 fusion.18
  19.5 0.6 fusion.17
  20.1 0.6 fusion.16
  20.7 0.6 fusion.15
  21.4 0.6 fusion.14
  22.0 0.6 fusion.13
  22.6 0.6 fusion.12
  23.2 0.6 fusion.11
  23.9 0.6 fusion.10
  24.5 0.6 fusion.9
  25.1 0.6 fusion.8
  25.7 23.9 %all-to-all-start = ((bf16[16,4,16,512]{3,2,1,0:T(8,128)(2,1)}), bf16[16,4,16,512]{3,2,1,0:T(8,128)(2,1)S(1)}, u32[]{:S(2)}, u32[]{:S(2)}) async-start(bf16[16,4,16,512]{3,2,1,0:T(8,128)(2,1)} %fusion.8), calls=%async_computation | async-start | bytes 2097152 | tf_op jit(solution)/shard_map/all_to_all | solution.py:58
  49.6 0.1 reduce-scatter.2.cloned.1.call-start
  49.7 0.0 copy-done.2
  49.7 0.1 dynamic_slice.7
  49.8 0.1 compare_and_fusion.2
  49.9 0.1 compare_convert_fusion
  50.0 32.7 %all-to-all-done = bf16[16,4,16,512]{3,2,1,0:T(8,128)(2,1)S(1)} async-done(((bf16[16,4,16,512]{3,2,1,0:T(8,128)(2,1)}), bf16[16,4,16,512]{3,2,1,0:T(8,128)(2,1)S(1)}, u32[]{:S(2)}, u32[]{:S(2)}) %all-to-all-start) | async-done | bytes 1048608 | tf_op jit(solution)/shard_map/all_to_all | solution.py:58
  82.7 0.6 gather_fusion.3
  83.2 0.0 all-gather.5.cloned.1.call-done
  83.3 2.1 gather_fusion.1
  85.4 0.3 fusion.2
  85.7 15.4 %all_gather.11 = bf16[4096,16]{0,1:T(8,128)(2,1)S(1)} all-gather(bf16[256,16]{0,1:T(8,128)(2,1)S(1)} %bitcast.108), channel_id=1, replica_groups=mesh['groups'=2,'adapter'=16,'tensor'=8] {'adapter'}, dimensions={0}, use_global_device_ids=true | all-gather | bytes 139264 | tf_op jit(solution)/shard_map/all_gather | solution.py:82
  101.2 4.5 %broadcast_multiply_fusion = f32[32,128,512]{2,1,0:T(8,128)} fusion(bf16[32,16,512]{2,1,0:T(8,128)(2,1)S(1)} %gather_fusion.3, pred[32]{0:T(512)(128)(4,1)S(1)} %get-tuple-element.7, bf16[4096,16]{0,1:T(8,128)(2,1)S(1)} %all_gather.11), kind=kOutput, calls=%fused_computation.6 | convolution fusion | flops 69468160 | bytes 9044000 | tf_op jit(solution)/shard_map/ksr,krf->ksf/dot_general | solution.py:85
  105.7 35.5 %all-gather.3.cloned.1.call-done = bf16[4096,1024]{1,0:T(8,128)(2,1)} async-done(((bf16[256,1024]{1,0:T(8,128)(2,1)}), bf16[4096,1024]{1,0:T(8,128)(2,1)}) %all-gather.3.cloned.1.call-update) | async-done | bytes 8388624 | tf_op jit(solution)/shard_map/all_gather | solution.py:81
  141.2 10.8 %fusion = bf16[4096,512]{1,0:T(8,128)(2,1)} fusion(f32[32,128,512]{2,1,0:T(8,128)} %broadcast_multiply_fusion, bf16[4096,1024]{1,0:T(8,128)(2,1)} %all-gather.3.cloned.1.call-done, bf16[1024,512]{1,0:T(8,128)(2,1)S(1)} %copy-done), kind=kOutput, calls=%fused_computation.5 | convolution fusion | flops 4299161600 | bytes 22020096 | tf_op jit(solution)/shard_map/dot_general | solution.py:83
  152.0 0.1 reduce-scatter.2.cloned.1.call-update
  152.0 55.6 %reduce-scatter.2.cloned.1.call-done = bf16[512,512]{1,0:T(8,128)(2,1)} async-done(((bf16[4096,512]{1,0:T(8,128)(2,1)}), bf16[512,512]{1,0:T(8,128)(2,1)}) %reduce-scatter.2.cloned.1.call-update) | async-done | bytes 524304 | tf_op jit(solution)/shard_map/reduce_scatter | solution.py:94
  (15 shorter events, 0.1 us)
Async XLA Ops:
  6.5 134.7 %copy-start = (bf16[1024,512]{1,0:T(8,128)(2,1)S(1)}, bf16[1024,512]{1,0:T(8,128)(2,1)}, u32[]{:S(2)}) copy-start(bf16[1024,512]{1,0:T(8,128)(2,1)} %param.8) | copy-start | bytes 3145732
  6.6 78.9 %copy-start.1 = (bf16[256,1024]{1,0:T(8,128)(2,1)S(1)}, bf16[256,1024]{1,0:T(8,128)(2,1)}, u32[]{:S(2)}) copy-start(bf16[256,1024]{1,0:T(8,128)(2,1)} %param.7) | copy-start | bytes 1572868
  6.6 43.1 %copy-start.2 = (s32[32]{0:T(128)S(1)}, s32[32]{0:T(128)}, u32[]{:S(2)}) copy-start(s32[32]{0:T(128)} %param.12) | copy-start | bytes 388
  6.6 76.7 %all-gather.5.cloned.1.call-start = ((), (), s32[]{:S(2)}) async-start(), calls=%async_computation.3 | async-start | bytes 2228224 | tf_op jit(solution)/shard_map/all_gather | solution.py:67
  10.8 130.4 %all-gather.3.cloned.1.call-start = ((), (), s32[]{:S(2)}) async-start(), calls=%async_computation.2 | async-start | bytes 8912896 | tf_op jit(solution)/shard_map/all_gather | solution.py:81
  25.7 56.9 %all-to-all-start = ((bf16[16,4,16,512]{3,2,1,0:T(8,128)(2,1)}), bf16[16,4,16,512]{3,2,1,0:T(8,128)(2,1)S(1)}, u32[]{:S(2)}, u32[]{:S(2)}) async-start(bf16[16,4,16,512]{3,2,1,0:T(8,128)(2,1)} %fusion.8), calls=%async_computation | async-start | bytes 2097152 | tf_op jit(solution)/shard_map/all_to_all | solution.py:58
  49.6 158.1 %reduce-scatter.2.cloned.1.call-start = ((), (), s32[]{:S(2)}) async-start(), calls=%async_computation.4 | async-start | bytes 4718592 | tf_op jit(solution)/shard_map/reduce_scatter | solution.py:94
Sparse Core Ops, SparseCore 0:
  10.9 72.3 all-gather.4
  85.1 56.0 all-gather.2
  152.2 55.4 reduce-scatter.1
